TPU v7x, 32 devices: a whole 2x2x4 slice. The times are simulated.
32 devices in a mesh: out: 8 (over z, y), inp: 4 (over x, core).
Axes of the slice: x: 2, y: 2, z: 4, core: 2. Of those that a mesh axis runs over, the one named last changes fastest.
Arguments:
- weight: float32 [8, 512, 13824], P(None, 'out', 'inp'), may hold values from -6 to 6
- gradient: bfloat16 [8, 512, 13824], P(None, 'out', 'inp'), may hold values from -60 to 60
- momentum: bfloat16 [8, 512, 13824], P(None, 'out', 'inp'), may hold values from -6 to 6
Outputs:
- weight_next: float32 [8, 512, 13824], P(None, 'out', 'inp')
- momentum_next: bfloat16 [8, 512, 13824], P(None, 'out', 'inp')
All inputs are finite; a program needn't handle non-finite values.
Results may differ from a plain program's by a relative error of at most 0.0039.
Values may be sent and summed in bfloat16 or wider, within the bound.
No kernel may reach another device: no remote copies, remote signals or barrier semaphores. Data moves between devices by JAX's collectives and lax.ppermute only.
A program may use at most 64 MiB of HBM per device.

v0:
```python
import math
import jax
import jax.numpy as jnp
from jax import lax
from jax.sharding import PartitionSpec as P

ITERS = 5
COLS = 13824
BETA = 0.95
EPSILON = 1e-06
COEF_A = 3.4445
COEF_B = -4.775
COEF_C = 2.0315


def mult(former, latter):
    return jnp.einsum("kij,kjl->kil", former, latter, precision=lax.Precision.HIGHEST)


def on_device(weight, gradient, momentum):
    moment = BETA * momentum.astype(jnp.float32) + gradient.astype(jnp.float32)
    source = (gradient.astype(jnp.float32) + BETA * moment).astype(jnp.bfloat16)
    local_squares = jnp.einsum("kic,kic->k", source, source, preferred_element_type=jnp.float32)
    totals = lax.psum(local_squares, ("out", "inp")) + EPSILON
    regrouped = lax.all_to_all(source, "out", split_axis=0, concat_axis=1, tiled=True)
    held = regrouped.shape[0]
    width = regrouped.shape[1]
    partial_value = jnp.einsum(
        "kic,kjc->kij", regrouped, regrouped, preferred_element_type=jnp.float32
    )
    scale2 = lax.dynamic_slice_in_dim(totals, lax.axis_index("out") * held, held, 0)
    gram = lax.psum(partial_value.astype(jnp.bfloat16), "inp").astype(jnp.float32)
    current = gram / scale2[:, None, None]
    transform = jnp.broadcast_to(jnp.eye(width, dtype=jnp.float32), (held, width, width))
    for sweep in range(ITERS):
        poly_part = COEF_B * current + COEF_C * mult(current, current)
        transform = COEF_A * transform + mult(poly_part, transform)
        halfway = COEF_A * current + mult(poly_part, current)
        current = COEF_A * halfway + mult(halfway, poly_part)
    factor = (transform / jnp.sqrt(scale2)[:, None, None]).astype(jnp.bfloat16)
    orthogonal = jnp.einsum("kij,kjc->kic", factor, regrouped, preferred_element_type=jnp.float32)
    update = (0.2 * math.sqrt(COLS) * orthogonal).astype(jnp.bfloat16)
    returned = lax.all_to_all(update, "out", split_axis=1, concat_axis=0, tiled=True)
    weight_next = 0.9 * weight - 0.5 * returned.astype(jnp.float32)
    return (weight_next, moment.astype(jnp.bfloat16))


def solution(mesh):
    return jax.shard_map(
        on_device,
        mesh=mesh,
        in_specs=(P(None, "out", "inp"), P(None, "out", "inp"), P(None, "out", "inp")),
        out_specs=(P(None, "out", "inp"), P(None, "out", "inp")),
        check_vma=False,
    )
```

profile of v0, /device:TPU:0, one launch (start us, length us, event | category | flops | bytes accessed | tf_op | source)
XLA Modules:
  0.0 335.9 jit_solution(17814851323513137917)
XLA Ops:
  7.2 4.2 %fusion.1 = (f32[8]{0:T(128)S(1)}, bf16[8,64,3456]{2,1,0:T(8,128)(2,1)S(1)}) fusion(bf16[8,64,3456]{2,1,0:T(8,128)(2,1)} %param.5, bf16[8,64,3456]{2,1,0:T(8,128)(2,1)} %param.4), kind=kLoop, calls=%fused_computation.4 | loop fusion | flops 17694712 | bytes 10616864 | tf_op jit(solution)/shard_map/kic,kic->k/dot_general | solution.py:23
  11.4 86.6 %all_to_all.8 = bf16[8,64,3456]{2,1,0:T(8,128)(2,1)S(1)} all-to-all(bf16[8,64,3456]{2,1,0:T(8,128)(2,1)S(1)} %get-tuple-element.3), channel_id=1, replica_groups=mesh['out'=8,'inp'=4] {'out'}, dimensions={0} | all-to-all | bytes 7077888 | tf_op jit(solution)/shard_map/all_to_all | solution.py:25
  98.0 2.9 fusion.29
  100.9 39.2 %psum.15 = f32[8]{0:T(128)S(1)} all-reduce(f32[8]{0:T(128)S(1)} %get-tuple-element.2), channel_id=1, replica_groups=mesh['out'=8,'inp'=4] {'out','inp'}, use_global_device_ids=true, to_apply=%region_1.0 | all-reduce | flops 8 | bytes 64 | tf_op jit(solution)/shard_map/psum | solution.py:24
  141.4 4.1 %fusion.11 = f32[512,512]{1,0:T(8,128)S(1)} fusion(bf16[1,512,512]{2,1,0:T(8,128)(2,1)} %all-reduce.2.cloned.1.call-done, f32[]{:T(128)} %bitcast.4), kind=kOutput, calls=%fused_computation.35 | convolution fusion | flops 1612447744 | bytes 1572868 | tf_op jit(solution)/shard_map/kij,kjl->kil/dot_general | solution.py:17
  146.5 2.6 fusion.12
  149.1 1.8 fusion.13
  150.9 1.9 fusion.15
  156.5 2.1 fusion.19
  166.1 1.9 fusion.23
  167.9 1.8 fusion.24
  169.8 2.1 convolution_add_fusion.1
  173.7 1.9 fusion.27
  175.6 1.9 fusion.28
  177.5 2.1 fusion.3
  179.7 19.5 %copy.14 = bf16[1,512,3456]{2,0,1:T(2,128)(2,1)} copy(bf16[1,512,3456]{2,1,0:T(8,128)(2,1)S(1)} %fusion.3) | data formatting | bytes 7077888 | tf_op jit(solution)/shard_map/convert_element_type | solution.py:42
  199.7 22.1 %reduce.2 = bf16[512,3456]{1,0:T(8,128)(2,1)S(1)} reduce(bf16[512,1,3456]{2,1,0:T(2,128)(2,1)} %bitcast.144, bf16[]{:T(256)} %broadcast.71), dimensions={1}, to_apply=%bitcast.143.reduce_sub_computation | reduce | bytes 7077890
  221.8 3.7 %reshape.156 = bf16[8,2,110592]{2,1,0:T(2,128)(2,1)} reshape(bf16[512,3456]{1,0:T(8,128)(2,1)S(1)} %reduce.2) | data formatting | bytes 7077888
  225.5 4.9 %all-to-all-start.1 = ((bf16[8,2,110592]{2,1,0:T(2,128)(2,1)}), bf16[8,2,110592]{2,1,0:T(2,128)(2,1)S(1)}, u32[]{:S(2)}, u32[]{:S(2)}) async-start(bf16[8,2,110592]{2,1,0:T(2,128)(2,1)} %reshape.156), calls=%async_computation.1 | async-start | bytes 7077888 | tf_op jit(solution)/shard_map/all_to_all | solution.py:43
  230.5 5.9 %fusion.2 = bf16[8,64,3456]{2,1,0:T(8,128)(2,1)} fusion(bf16[8,64,3456]{2,1,0:T(8,128)(2,1)} %param.4, bf16[8,64,3456]{2,1,0:T(8,128)(2,1)} %param.5), kind=kLoop, calls=%fused_computation.7 | loop fusion | flops 8847360 | bytes 10616832 | tf_op jit(solution)/shard_map/convert_element_type | solution.py:45
  236.4 72.2 %all-to-all-done.1 = bf16[8,2,110592]{2,1,0:T(2,128)(2,1)S(1)} async-done(((bf16[8,2,110592]{2,1,0:T(2,128)(2,1)}), bf16[8,2,110592]{2,1,0:T(2,128)(2,1)S(1)}, u32[]{:S(2)}, u32[]{:S(2)}) %all-to-all-start.1) | async-done | bytes 3538976 | tf_op jit(solution)/shard_map/all_to_all | solution.py:43
  308.6 5.5 %reshape.157 = bf16[512,1,3456]{2,1,0:T(2,128)(2,1)} reshape(bf16[8,2,110592]{2,1,0:T(2,128)(2,1)S(1)} %all-to-all-done.1) | data formatting | bytes 7077888
  314.1 9.0 %convert_multiply_fusion.1 = f32[1,512,3456]{2,0,1:T(1,128)S(1)} fusion(bf16[512,1,3456]{2,1,0:T(2,128)(2,1)} %reshape.157), kind=kLoop, calls=%fused_computation.5 | loop fusion | flops 3538944 | bytes 10616832 | tf_op jit(solution)/shard_map/mul | solution.py:44
  325.0 3.9 %multiply_subtract_fusion = f32[8,64,3456]{2,1,0:T(8,128)} fusion(f32[8,64,3456]{2,1,0:T(8,128)S(1)} %bitcast.145, f32[8,64,3456]{2,1,0:T(8,128)S(1)} %bitcast.147), kind=kLoop, calls=%fused_computation.8 | loop fusion | flops 3538944 | bytes 21233664 | tf_op jit(solution)/shard_map/sub | solution.py:44
  (22 shorter events, 16.9 us)
Async XLA Ops:
  7.2 134.3 %all-reduce.2.cloned.1.call-start = ((), (), s32[]{:S(2)}) async-start(), calls=%async_computation.2 | async-start | bytes 1048576 | tf_op jit(solution)/shard_map/psum | solution.py:32
  141.4 5.1 %copy-start = (bf16[1,512,512]{2,1,0:T(8,128)(2,1)S(1)}, bf16[1,512,512]{2,1,0:T(8,128)(2,1)}, u32[]{:S(2)}) copy-start(bf16[1,512,512]{2,1,0:T(8,128)(2,1)} %all-reduce.2.cloned.1.call-done) | copy-start | bytes 1572868
  225.5 83.0 %all-to-all-start.1 = ((bf16[8,2,110592]{2,1,0:T(2,128)(2,1)}), bf16[8,2,110592]{2,1,0:T(2,128)(2,1)S(1)}, u32[]{:S(2)}, u32[]{:S(2)}) async-start(bf16[8,2,110592]{2,1,0:T(2,128)(2,1)} %reshape.156), calls=%async_computation.1 | async-start | bytes 7077888 | tf_op jit(solution)/shard_map/all_to_all | solution.py:43
  314.1 9.5 %slice-start = ((s8[7077888]{0:T(1024)(128)(4,1)}), s8[4194304]{0:T(1024)(128)(4,1)S(1)}, s32[]{:S(2)}) async-start(s8[7077888]{0:T(1024)(128)(4,1)} %bitcast.146), calls=%async_computation.3 | async-start | bytes 8388608
  323.1 1.8 slice-start.1
Sparse Core Ops, SparseCore 0:
  101.0 32.2 all-reduce.1
where the time goes:
time: 339 us; the launch traced here: 336 us
  blocking collectives  126 us (37%)
  waiting for transfers between devices  72.2 us (21%)
  other arithmetic  45.2 us (13%)
  matrix products  40.9 us (12%)
  local copies, waits for them, and re-layouts  31.6 us (9%)
  between operations  15.2 us (4%)
  starting transfers between devices  4.98 us (1%)
    all_to_all x1, blocking collectives, on_device(): lax.all_to_all(source, 'out', split_axis=0, concat_axis=1, tiled=True)  86.6 us
    all_to_all x1, waiting for transfers between devices, on_device(): lax.all_to_all(update, 'out', split_axis=1, concat_axis=0, tiled=True)  72.2 us
    psum x1, blocking collectives, on_device(): totals = lax.psum(local_squares, ('out', 'inp')) + EPSILON  39.2 us
    dot_general x18, matrix products, mult(): jnp.einsum('kij,kjl->kil', former, latter, precision=lax.Precision.HIGHEST)  36 us
    unnamed x2, other arithmetic  22.1 us
    convert_element_type x1, local copies, waits for them, and re-layouts, on_device(): update = (0.2 * math.sqrt(COLS) * orthogonal).astype(jnp.bfloat16)  19.5 us
    unnamed x10, local copies, waits for them, and re-layouts  11.6 us
    mul x1, other arithmetic, on_device(): weight_next = 0.9 * weight - 0.5 * returned.astype(jnp.float32)  9.03 us
  transfers between devices with their start and end apart: 2, of which 1 were waited for; matrix products, arithmetic and copies ran while one was open for 2% of the time, Pallas kernels for 0%

commit v1 on v0

--- a/solution.py
+++ b/solution.py
@@ -11,6 +11,28 @@
 COEF_A = 3.4445
 COEF_B = -4.775
 COEF_C = 2.0315
+
+
+def cut_along(x, dim, size):
+    before, after = (x.shape[:dim], x.shape[dim + 1 :])
+    return jnp.moveaxis(x.reshape(*before, size, -1, *after), dim, 0)
+
+
+def in_order(parts, dim):
+    parts = jnp.moveaxis(parts, 0, dim)
+    lengths = parts.shape
+    return parts.reshape(*lengths[:dim], lengths[dim] * lengths[dim + 1], *lengths[dim + 2 :])
+
+
+def exchange_in_pairs(x, axis, split_dim, concat_dim):
+    size, here = (lax.axis_size(axis), lax.axis_index(axis))
+    blocks = cut_along(x, split_dim, size)
+    outs = [blocks[here]]
+    for step in range(1, size):
+        sent = blocks[here ^ step]
+        outs.append(lax.ppermute(sent, axis, [(i, i ^ step) for i in range(size)]))
+    blocks = jnp.stack(outs)[here ^ jnp.arange(size)]
+    return in_order(blocks, concat_dim)
 
 
 def mult(former, latter):
@@ -40,7 +62,7 @@
     factor = (transform / jnp.sqrt(scale2)[:, None, None]).astype(jnp.bfloat16)
     orthogonal = jnp.einsum("kij,kjc->kic", factor, regrouped, preferred_element_type=jnp.float32)
     update = (0.2 * math.sqrt(COLS) * orthogonal).astype(jnp.bfloat16)
-    returned = lax.all_to_all(update, "out", split_axis=1, concat_axis=0, tiled=True)
+    returned = exchange_in_pairs(update, "out", 1, 0)
     weight_next = 0.9 * weight - 0.5 * returned.astype(jnp.float32)
     return (weight_next, moment.astype(jnp.bfloat16))
 

time: 339 us -> 287 us (0.85)
  the two profiles are of different devices: /device:TPU:0 before, /device:TPU:10 now
where the time goes in v1:
time: 287 us; the launch traced here: 284 us
  blocking collectives  125 us (44%)
  waiting for transfers between devices  70.8 us (25%)
  matrix products  41.3 us (14%)
  between operations  15.3 us (5%)
  other arithmetic  14 us (5%)
  starting transfers between devices  9.7 us (3%)
  local copies, waits for them, and re-layouts  7.72 us (3%)
    all_to_all x1, blocking collectives, on_device(): lax.all_to_all(source, 'out', split_axis=0, concat_axis=1, tiled=True)  84.4 us
    ppermute x7, waiting for transfers between devices, exchange_in_pairs(): outs.append(lax.ppermute(sent, axis, [(i, i ^ step) for i in range(size)]))  70.8 us
    psum x1, blocking collectives, on_device(): totals = lax.psum(local_squares, ('out', 'inp')) + EPSILON  40.6 us
    dot_general x18, matrix products, mult(): jnp.einsum('kij,kjl->kil', former, latter, precision=lax.Precision.HIGHEST)  36.3 us
    ppermute x7, starting transfers between devices, exchange_in_pairs(): outs.append(lax.ppermute(sent, axis, [(i, i ^ step) for i in range(size)]))  9.66 us
    sub x1, other arithmetic, on_device(): weight_next = 0.9 * weight - 0.5 * returned.astype(jnp.float32)  6.9 us
  transfers between devices with their start and end apart: 8, of which 5 were waited for; matrix products, arithmetic and copies ran while one was open for 1% of the time, Pallas kernels for 0%

profile of v1, /device:TPU:10, one launch (start us, length us, event | category | flops | bytes accessed | tf_op | source)
XLA Modules:
  0.0 283.9 jit_solution(2307529159286097660)
XLA Ops:
  7.2 4.2 %fusion.1 = (f32[8]{0:T(128)S(1)}, bf16[8,64,3456]{2,1,0:T(8,128)(2,1)S(1)}) fusion(bf16[8,64,3456]{2,1,0:T(8,128)(2,1)} %param.5, bf16[8,64,3456]{2,1,0:T(8,128)(2,1)} %param.4), kind=kLoop, calls=%fused_computation.5 | loop fusion | flops 17694712 | bytes 10616864 | tf_op jit(solution)/shard_map/kic,kic->k/dot_general | solution.py:45
  11.4 84.4 %all_to_all.4 = bf16[8,64,3456]{2,1,0:T(8,128)(2,1)S(1)} all-to-all(bf16[8,64,3456]{2,1,0:T(8,128)(2,1)S(1)} %get-tuple-element.3), channel_id=1, replica_groups=mesh['out'=8,'inp'=4] {'out'}, dimensions={0} | all-to-all | bytes 7077888 | tf_op jit(solution)/shard_map/all_to_all | solution.py:47
  95.9 2.9 %fusion.28 = bf16[1,512,512]{2,1,0:T(8,128)(2,1)} fusion(bf16[512,3456]{1,0:T(8,128)(2,1)S(1)} %bitcast.169), kind=kOutput, calls=%fused_computation.53 | convolution fusion | flops 1812201472 | bytes 4063232 | tf_op jit(solution)/shard_map/kic,kjc->kij/dot_general | solution.py:50
  98.8 40.6 %psum.15 = f32[8]{0:T(128)S(1)} all-reduce(f32[8]{0:T(128)S(1)} %get-tuple-element.2), channel_id=1, replica_groups=mesh['out'=8,'inp'=4] {'out','inp'}, use_global_device_ids=true, to_apply=%region_1.0 | all-reduce | flops 8 | bytes 64 | tf_op jit(solution)/shard_map/psum | solution.py:46
  140.8 4.2 %fusion.10 = f32[512,512]{1,0:T(8,128)S(1)} fusion(bf16[1,512,512]{2,1,0:T(8,128)(2,1)} %all-reduce.2.cloned.1.call-done, f32[]{:T(128)} %bitcast.4), kind=kOutput, calls=%fused_computation.34 | convolution fusion | flops 1612447744 | bytes 1572868 | tf_op jit(solution)/shard_map/kij,kjl->kil/dot_general | solution.py:39
  146.0 2.6 fusion.11
  156.1 2.0 fusion.16
  165.6 1.9 fusion.22
  167.5 1.9 fusion.23
  169.4 2.1 convolution_add_fusion.1
  173.4 1.9 fusion.26
  175.3 1.9 fusion.27
  177.2 2.1 multiply_convert_fusion
  182.5 2.9 %fusion.2 = bf16[8,64,3456]{2,1,0:T(8,128)(2,1)} fusion(bf16[8,64,3456]{2,1,0:T(8,128)(2,1)S(1)} %copy-done.1, bf16[8,64,3456]{2,1,0:T(8,128)(2,1)S(1)} %copy-done), kind=kLoop, calls=%fused_computation.8 | loop fusion | flops 8847360 | bytes 10616832 | tf_op jit(solution)/shard_map/convert_element_type | solution.py:67
  185.8 2.0 collective-permute-start.2
  188.8 2.5 collective-permute-start.4
  191.9 20.9 %collective-permute-done.1 = bf16[1,64,3456]{2,1,0:T(8,128)(2,1)S(1)} collective-permute-done((bf16[1,64,3456]{2,1,0:T(8,128)(2,1)S(1)}, bf16[1,64,3456]{2,1,0:T(8,128)(2,1)S(1)}, u32[]{:S(2)}, u32[]{:S(2)}) %collective-permute-start.1) | collective-permute-done | bytes 442400 | tf_op jit(solution)/shard_map/ppermute | solution.py:33
  212.8 2.1 collective-permute-start.6
  215.0 5.3 %collective-permute-done.2 = bf16[1,64,3456]{2,1,0:T(8,128)(2,1)S(1)} collective-permute-done((bf16[1,64,3456]{2,1,0:T(8,128)(2,1)S(1)}, bf16[1,64,3456]{2,1,0:T(8,128)(2,1)S(1)}, u32[]{:S(2)}, u32[]{:S(2)}) %collective-permute-start.2) | collective-permute-done | bytes 442400 | tf_op jit(solution)/shard_map/ppermute | solution.py:33
  220.4 26.3 %collective-permute-done.4 = bf16[1,64,3456]{2,1,0:T(8,128)(2,1)S(1)} collective-permute-done((bf16[1,64,3456]{2,1,0:T(8,128)(2,1)S(1)}, bf16[1,64,3456]{2,1,0:T(8,128)(2,1)S(1)}, u32[]{:S(2)}, u32[]{:S(2)}) %collective-permute-start.4) | collective-permute-done | bytes 442400 | tf_op jit(solution)/shard_map/ppermute | solution.py:33
  246.8 11.3 %collective-permute-done.5 = bf16[1,64,3456]{2,1,0:T(8,128)(2,1)S(1)} collective-permute-done((bf16[1,64,3456]{2,1,0:T(8,128)(2,1)S(1)}, bf16[1,64,3456]{2,1,0:T(8,128)(2,1)S(1)}, u32[]{:S(2)}, u32[]{:S(2)}) %collective-permute-start.5) | collective-permute-done | bytes 442400 | tf_op jit(solution)/shard_map/ppermute | solution.py:33
  258.1 7.0 %collective-permute-done.6 = bf16[1,64,3456]{2,1,0:T(8,128)(2,1)S(1)} collective-permute-done((bf16[1,64,3456]{2,1,0:T(8,128)(2,1)S(1)}, bf16[1,64,3456]{2,1,0:T(8,128)(2,1)S(1)}, u32[]{:S(2)}, u32[]{:S(2)}) %collective-permute-start.6) | collective-permute-done | bytes 442400 | tf_op jit(solution)/shard_map/ppermute | solution.py:33
  266.9 3.0 %gather_fusion = bf16[8,64,3456]{2,1,0:T(8,128)(2,1)S(1)} fusion(bf16[8,64,3456]{2,1,0:T(8,128)(2,1)} %bitcast.168, s32[1024]{0:T(1024)S(1)} %pad_clamp_fusion), kind=kCustom, calls=%fused_computation | custom fusion | bytes 7077920 | tf_op jit(solution)/shard_map/gather | solution.py:34
  270.0 6.9 %multiply_subtract_fusion = f32[8,64,3456]{2,1,0:T(8,128)} fusion(bf16[8,64,3456]{2,1,0:T(8,128)(2,1)S(1)} %gather_fusion, f32[8,64,3456]{2,1,0:T(8,128)} %param.3), kind=kLoop, calls=%fused_computation.6 | loop fusion | flops 7077888 | bytes 17694720 | tf_op jit(solution)/shard_map/sub | solution.py:66
  (39 shorter events, 25.5 us)
Async XLA Ops:
  7.2 133.6 %all-reduce.2.cloned.1.call-start = ((), (), s32[]{:S(2)}) async-start(), calls=%async_computation.1 | async-start | bytes 1048576 | tf_op jit(solution)/shard_map/psum | solution.py:54
  140.8 5.2 %copy-start.3 = (bf16[1,512,512]{2,1,0:T(8,128)(2,1)S(1)}, bf16[1,512,512]{2,1,0:T(8,128)(2,1)}, u32[]{:S(2)}) copy-start(bf16[1,512,512]{2,1,0:T(8,128)(2,1)} %all-reduce.2.cloned.1.call-done) | copy-start | bytes 1572868
  179.4 2.0 copy-start
  179.4 3.1 %copy-start.1 = (bf16[8,64,3456]{2,1,0:T(8,128)(2,1)S(1)}, bf16[8,64,3456]{2,1,0:T(8,128)(2,1)}, u32[]{:S(2)}) copy-start(bf16[8,64,3456]{2,1,0:T(8,128)(2,1)} %param.4) | copy-start | bytes 10616836
  179.7 11.6 %collective-permute-start = (bf16[1,64,3456]{2,1,0:T(8,128)(2,1)S(1)}, bf16[1,64,3456]{2,1,0:T(8,128)(2,1)S(1)}, u32[]{:S(2)}, u32[]{:S(2)}) collective-permute-start(bf16[1,64,3456]{2,1,0:T(8,128)(2,1)S(1)} %get-tuple-element.10), channel_id=1, source_target_pairs={{0,4},{4,0},{8,12},{12,8},{16,20},{20,16},{24,28},{28,24},{1,5},{5... | collective-permute-start | bytes 1327112 | tf_op jit(solution)/shard_map/ppermute | solution.py:33
  185.4 27.5 %collective-permute-start.1 = (bf16[1,64,3456]{2,1,0:T(8,128)(2,1)S(1)}, bf16[1,64,3456]{2,1,0:T(8,128)(2,1)S(1)}, u32[]{:S(2)}, u32[]{:S(2)}) collective-permute-start(bf16[1,64,3456]{2,1,0:T(8,128)(2,1)S(1)} %get-tuple-element.9), channel_id=1, source_target_pairs={{0,8},{4,12},{8,0},{12,4},{16,24},{20,28},{24,16},{28,20},{1,9},{5... | collective-permute-start | bytes 1327112 | tf_op jit(solution)/shard_map/ppermute | solution.py:33
  185.8 34.5 %collective-permute-start.2 = (bf16[1,64,3456]{2,1,0:T(8,128)(2,1)S(1)}, bf16[1,64,3456]{2,1,0:T(8,128)(2,1)S(1)}, u32[]{:S(2)}, u32[]{:S(2)}) collective-permute-start(bf16[1,64,3456]{2,1,0:T(8,128)(2,1)S(1)} %get-tuple-element.8), channel_id=1, source_target_pairs={{0,12},{4,8},{8,4},{12,0},{16,28},{20,24},{24,20},{28,16},{1,13},{... | collective-permute-start | bytes 1327112 | tf_op jit(solution)/shard_map/ppermute | solution.py:33
  187.8 32.5 %collective-permute-start.3 = (bf16[1,64,3456]{2,1,0:T(8,128)(2,1)S(1)}, bf16[1,64,3456]{2,1,0:T(8,128)(2,1)S(1)}, u32[]{:S(2)}, u32[]{:S(2)}) collective-permute-start(bf16[1,64,3456]{2,1,0:T(8,128)(2,1)S(1)} %get-tuple-element.7), channel_id=1, source_target_pairs={{0,16},{4,20},{8,24},{12,28},{16,0},{20,4},{24,8},{28,12},{1,17},{... | collective-permute-start | bytes 1327112 | tf_op jit(solution)/shard_map/ppermute | solution.py:33
  188.8 58.0 %collective-permute-start.4 = (bf16[1,64,3456]{2,1,0:T(8,128)(2,1)S(1)}, bf16[1,64,3456]{2,1,0:T(8,128)(2,1)S(1)}, u32[]{:S(2)}, u32[]{:S(2)}) collective-permute-start(bf16[1,64,3456]{2,1,0:T(8,128)(2,1)S(1)} %get-tuple-element.6), channel_id=1, source_target_pairs={{0,20},{4,16},{8,28},{12,24},{16,4},{20,0},{24,12},{28,8},{1,21},{... | collective-permute-start | bytes 1327112 | tf_op jit(solution)/shard_map/ppermute | solution.py:33
  191.3 66.8 %collective-permute-start.5 = (bf16[1,64,3456]{2,1,0:T(8,128)(2,1)S(1)}, bf16[1,64,3456]{2,1,0:T(8,128)(2,1)S(1)}, u32[]{:S(2)}, u32[]{:S(2)}) collective-permute-start(bf16[1,64,3456]{2,1,0:T(8,128)(2,1)S(1)} %get-tuple-element.5), channel_id=1, source_target_pairs={{0,24},{4,28},{8,16},{12,20},{16,8},{20,12},{24,0},{28,4},{1,25},{... | collective-permute-start | bytes 1327112 | tf_op jit(solution)/shard_map/ppermute | solution.py:33
  212.8 52.2 %collective-permute-start.6 = (bf16[1,64,3456]{2,1,0:T(8,128)(2,1)S(1)}, bf16[1,64,3456]{2,1,0:T(8,128)(2,1)S(1)}, u32[]{:S(2)}, u32[]{:S(2)}) collective-permute-start(bf16[1,64,3456]{2,1,0:T(8,128)(2,1)S(1)} %get-tuple-element.4), channel_id=1, source_target_pairs={{0,28},{4,24},{8,20},{12,16},{16,12},{20,8},{24,4},{28,0},{1,29},{... | collective-permute-start | bytes 1327112 | tf_op jit(solution)/shard_map/ppermute | solution.py:33
  265.1 1.8 copy-start.2
Sparse Core Ops, SparseCore 0:
  98.9 31.7 all-reduce.1
